TPU v7x, 32 devices: a whole 2x2x4 slice. The times are simulated.
32 devices in a mesh: seq: 8 (over z, x), head: 4 (over y, core).
Axes of the slice: x: 2, y: 2, z: 4, core: 2. Of those that a mesh axis runs over, the one named last changes fastest.
Arguments:
- queries: bfloat16 [2048, 4096], P('seq', 'head'), may hold values from -48 to 48
- key_rows: bfloat16 [2048, 4096], P('seq', 'head'), may hold values from -4 to 4
- value_rows: bfloat16 [2048, 4096], P('seq', 'head'), may hold values from -6 to 6
- out_grad: bfloat16 [2048, 2048], P('seq', 'head'), may hold values from -6 to 6
- out_proj: bfloat16 [4096, 2048], P('head'), may hold values from -0.125 to 0.125
- section_table: int32 [32, 3], P('head'), may hold values 0 or 1
- block_active: int32 [8, 3], P('seq'), may hold values 0 or 1
Outputs:
- query_grad: bfloat16 [2048, 4096], P('seq', 'head')
- key_grad: bfloat16 [2048, 4096], P('seq', 'head')
- value_grad: bfloat16 [2048, 4096], P('seq', 'head')
All inputs are finite; a program needn't handle non-finite values.
Results may differ from a plain program's by a relative error of at most 0.008.
Values may be sent and summed in bfloat16 or wider, within the bound.
A program may use at most 64 MiB of HBM per device.

v0:
```python
from functools import reduce
import math

import jax
import jax.numpy as jnp
from jax import lax
from jax.sharding import PartitionSpec as P

BLK = 256
HDIM = 128
SECTIONS = 3


def shifted(value, axis, steps):
    count = lax.axis_size(axis)
    initial, last = (max(0, -steps), min(count, count - steps))
    return lax.ppermute(value, axis, [(source, source + steps) for source in range(initial, last)])


def split_heads(matrix):
    row_count, col_count = matrix.shape
    return matrix.reshape(row_count // BLK, BLK, col_count // HDIM, HDIM)


def join_heads(blocks):
    block_count, block_rows, head_count, head_size = blocks.shape
    return blocks.reshape(block_count * block_rows, head_count * head_size)


def body(queries, key_rows, value_rows, out_grad, out_proj, section_table, block_active):
    score_scale = 1.0 / math.sqrt(HDIM)
    seq_count = lax.axis_size("seq")
    position = lax.axis_index("seq")
    span_list = [seq_count // 2 ** (section_index + 1) for section_index in range(SECTIONS)]
    hop_list = [
        span_list[section_index]
        - (span_list[section_index + 1] if section_index + 1 < SECTIONS else 0)
        for section_index in range(SECTIONS)
    ]
    attn_grad = lax.dot_general(
        lax.all_gather(out_grad, "head", axis=1, tiled=True),
        out_proj,
        (((1,), (1,)), ((), ())),
        preferred_element_type=jnp.float32,
    ).astype(jnp.bfloat16)
    remote = [None] * SECTIONS
    carry_keys = key_rows
    carry_values = value_rows
    for section_index in reversed(range(SECTIONS)):
        carry_keys, carry_values = shifted(
            (carry_keys, carry_values), "seq", hop_list[section_index]
        )
        remote[section_index] = (carry_keys, carry_values)
    query_blocks = split_heads(queries)
    grad_blocks = split_heads(attn_grad)
    row_index = lax.broadcasted_iota(jnp.int32, (BLK, BLK), 0)
    col_index = lax.broadcasted_iota(jnp.int32, (BLK, BLK), 1)
    causal = (row_index >= col_index)[None, None]
    key_sets = [(split_heads(key_rows), split_heads(value_rows), causal)]
    for section_index in range(SECTIONS):
        usable = (
            section_table[:, section_index][None, :] * block_active[:, section_index][:, None] > 0
        ) & (position >= span_list[section_index])
        key_sets.append(
            (
                split_heads(remote[section_index][0]),
                split_heads(remote[section_index][1]),
                usable[:, :, None, None],
            )
        )
    logits = []
    for key_entry in key_sets:
        raw_scores = (
            jnp.einsum(
                "bihd,bjhd->bhij", query_blocks, key_entry[0], preferred_element_type=jnp.float32
            )
            * score_scale
        )
        logits.append(jnp.where(key_entry[2], raw_scores, -1e30))
    row_max = reduce(jnp.maximum, [jnp.max(logit_set, axis=-1) for logit_set in logits])
    row_sum = reduce(
        jnp.add, [jnp.sum(jnp.exp(logit_set - row_max[..., None]), axis=-1) for logit_set in logits]
    )
    log_norm = row_max + jnp.log(row_sum)
    probs_list = [
        jnp.where(key_entry[2], jnp.exp(logit_set - log_norm[..., None]), 0.0)
        for logit_set, key_entry in zip(logits, key_sets)
    ]
    weight_list = [prob_set.astype(jnp.bfloat16) for prob_set in probs_list]
    context = reduce(
        jnp.add,
        [
            jnp.einsum(
                "bhij,bjhd->bihd", weight_set, key_entry[1], preferred_element_type=jnp.float32
            )
            for weight_set, key_entry in zip(weight_list, key_sets)
        ],
    )
    row_delta = jnp.swapaxes(jnp.sum(grad_blocks.astype(jnp.float32) * context, axis=-1), 1, 2)
    query_sum = jnp.zeros(query_blocks.shape, jnp.float32)
    partials = []
    for set_index in range(SECTIONS + 1):
        key_part, value_part, allowed = key_sets[set_index]
        prob_grad = jnp.einsum(
            "bihd,bjhd->bhij", grad_blocks, value_part, preferred_element_type=jnp.float32
        )
        dlogit = (probs_list[set_index] * (prob_grad - row_delta[..., None]) * score_scale).astype(
            jnp.bfloat16
        )
        query_sum = query_sum + jnp.einsum(
            "bhij,bjhd->bihd", dlogit, key_part, preferred_element_type=jnp.float32
        )
        key_term = join_heads(
            jnp.einsum("bhij,bihd->bjhd", dlogit, query_blocks, preferred_element_type=jnp.float32)
        )
        value_term = join_heads(
            jnp.einsum(
                "bhij,bihd->bjhd",
                weight_list[set_index],
                grad_blocks,
                preferred_element_type=jnp.float32,
            )
        )
        if set_index > 0:
            key_term = key_term.astype(jnp.bfloat16)
            value_term = value_term.astype(jnp.bfloat16)
        partials.append((key_term, value_term))
    key_sum, value_sum = partials[0]
    for section_index in range(SECTIONS):
        key_back, value_back = shifted(
            (partials[section_index + 1][0], partials[section_index + 1][1]),
            "seq",
            -span_list[section_index],
        )
        key_sum = key_sum + key_back.astype(jnp.float32)
        value_sum = value_sum + value_back.astype(jnp.float32)
    return (
        join_heads(query_sum).astype(jnp.bfloat16),
        key_sum.astype(jnp.bfloat16),
        value_sum.astype(jnp.bfloat16),
    )


def solution(mesh):
    return jax.shard_map(
        body,
        mesh=mesh,
        in_specs=(
            P("seq", "head"),
            P("seq", "head"),
            P("seq", "head"),
            P("seq", "head"),
            P("head", None),
            P("head", None),
            P("seq", None),
        ),
        out_specs=(P("seq", "head"), P("seq", "head"), P("seq", "head")),
        check_vma=False,
    )
```

profile of v0, /device:TPU:0, one launch (start us, length us, event | category | flops | bytes accessed | tf_op | source)
XLA Modules:
  0.0 228.0 jit_solution(5760111906565373100)
XLA Ops:
  8.5 5.7 %collective-permute-start = (bf16[256,1024]{0,1:T(8,128)(2,1)S(1)}, bf16[256,1024]{0,1:T(8,128)(2,1)}, u32[]{:S(2)}, u32[]{:S(2)}) collective-permute-start(bf16[256,1024]{0,1:T(8,128)(2,1)S(1)} %copy.156), channel_id=1, source_target_pairs={{0,4},{4,8},{8,12},{12,16},{16,20},{20,24},{24,28},{1,5},{5,9},{9,... | collective-permute-start | bytes 1572872 | tf_op jit(solution)/shard_map/ppermute | solution.py:17
  14.2 3.5 %collective-permute-start.3 = (bf16[256,1024]{1,0:T(8,128)(2,1)}, bf16[256,1024]{1,0:T(8,128)(2,1)}, u32[]{:S(2)}, u32[]{:S(2)}) collective-permute-start(bf16[256,1024]{1,0:T(8,128)(2,1)} %param.9), channel_id=1, source_target_pairs={{0,4},{4,8},{8,12},{12,16},{16,20},{20,24},{24,28},{1,5},{5,9},{9,... | collective-permute-start | bytes 1572872 | tf_op jit(solution)/shard_map/ppermute | solution.py:17
  17.8 2.0 copy.159
  20.7 5.1 %collective-permute-done = bf16[256,1024]{0,1:T(8,128)(2,1)} collective-permute-done((bf16[256,1024]{0,1:T(8,128)(2,1)S(1)}, bf16[256,1024]{0,1:T(8,128)(2,1)}, u32[]{:S(2)}, u32[]{:S(2)}) %collective-permute-start) | collective-permute-done | bytes 524320 | tf_op jit(solution)/shard_map/ppermute | solution.py:17
  25.7 5.3 %collective-permute-start.1 = (bf16[256,1024]{0,1:T(8,128)(2,1)}, bf16[256,1024]{0,1:T(8,128)(2,1)}, u32[]{:S(2)}, u32[]{:S(2)}) collective-permute-start(bf16[256,1024]{0,1:T(8,128)(2,1)} %collective-permute-done), channel_id=1, source_target_pairs={{0,4},{4,8},{8,12},{12,16},{16,20},{20,24},{24,28},{1,5},{5,9},{9,... | collective-permute-start | bytes 1572872 | tf_op jit(solution)/shard_map/ppermute | solution.py:17
  31.6 5.5 %collective-permute-done.3 = bf16[256,1024]{1,0:T(8,128)(2,1)} collective-permute-done((bf16[256,1024]{1,0:T(8,128)(2,1)}, bf16[256,1024]{1,0:T(8,128)(2,1)}, u32[]{:S(2)}, u32[]{:S(2)}) %collective-permute-start.3) | collective-permute-done | bytes 524320 | tf_op jit(solution)/shard_map/ppermute | solution.py:17
  37.0 5.2 %collective-permute-start.4 = (bf16[256,1024]{1,0:T(8,128)(2,1)}, bf16[256,1024]{1,0:T(8,128)(2,1)}, u32[]{:S(2)}, u32[]{:S(2)}) collective-permute-start(bf16[256,1024]{1,0:T(8,128)(2,1)} %collective-permute-done.3), channel_id=1, source_target_pairs={{0,4},{4,8},{8,12},{12,16},{16,20},{20,24},{24,28},{1,5},{5,9},{9,... | collective-permute-start | bytes 1572872 | tf_op jit(solution)/shard_map/ppermute | solution.py:17
  42.2 1.9 and_bitcast_fusion.2
  44.2 2.0 copy.86
  46.2 2.1 collective-permute-done.1
  48.3 5.4 %collective-permute-start.2 = (bf16[256,1024]{0,1:T(8,128)(2,1)}, bf16[256,1024]{0,1:T(8,128)(2,1)S(1)}, u32[]{:S(2)}, u32[]{:S(2)}) collective-permute-start(bf16[256,1024]{0,1:T(8,128)(2,1)} %collective-permute-done.1), channel_id=1, source_target_pairs={{0,8},{4,12},{8,16},{12,20},{16,24},{20,28},{1,9},{5,13},{9,17},{1... | collective-permute-start | bytes 1572872 | tf_op jit(solution)/shard_map/ppermute | solution.py:17
  53.7 2.9 %fusion.24 = (f32[8,256]{1,0:T(8,128)S(1)}, f32[8,256,256]{1,2,0:T(8,128)}) fusion(bf16[256,8,128]{0,2,1:T(8,128)(2,1)S(1)} %bitcast.133, bf16[256,8,128]{0,2,1:T(8,128)(2,1)} %bitcast.8, pred[8]{0:T(512)(128)(4,1)S(1)} %get-tuple-element.14), kind=kOutput, calls=%fused_computation.51 | convolution fusion | flops 135788544 | bytes 3153928 | tf_op jit(solution)/shard_map/bihd,bjhd->bhij/dot_general | solution.py:74
  58.4 7.3 %collective-permute-start.5 = (bf16[256,1024]{1,0:T(8,128)(2,1)}, bf16[256,1024]{1,0:T(8,128)(2,1)}, u32[]{:S(2)}, u32[]{:S(2)}) collective-permute-start(bf16[256,1024]{1,0:T(8,128)(2,1)} %collective-permute-done.4), channel_id=1, source_target_pairs={{0,8},{4,12},{8,16},{12,20},{16,24},{20,28},{1,9},{5,13},{9,17},{1... | collective-permute-start | bytes 1572872 | tf_op jit(solution)/shard_map/ppermute | solution.py:17
  65.7 2.1 copy.84
  67.8 2.9 %fusion.25 = (f32[8,256]{1,0:T(8,128)S(1)}, f32[8,256,256]{1,2,0:T(8,128)}) fusion(bf16[256,8,128]{0,2,1:T(8,128)(2,1)S(1)} %bitcast.134, bf16[256,8,128]{0,2,1:T(8,128)(2,1)} %bitcast.5, pred[8]{0:T(512)(128)(4,1)S(1)} %get-tuple-element.15), kind=kOutput, calls=%fused_computation.52 | convolution fusion | flops 135788544 | bytes 3153928 | tf_op jit(solution)/shard_map/bihd,bjhd->bhij/dot_general | solution.py:74
  75.7 4.5 %exponential_reduce_fusion.2 = (f32[8,256]{1,0:T(8,128)S(1)}, f32[8,256]{1,0:T(8,128)S(1)}, f32[8,256]{1,0:T(8,128)S(1)}, f32[8,256]{1,0:T(8,128)S(1)}) fusion(f32[8,256,256]{1,2,0:T(8,128)} %get-tuple-element.26, f32[8,256]{1,0:T(8,128)S(1)} %maximum_maximum_fusion, f32[8,256,256]{1,2,0:T(8,128)} %get-tuple-element.22, ...), kind=kLoop, calls=%fused_computation.10 | loop fusion | flops 4186112 | bytes 8429568 | tf_op jit(solution)/shard_map/reduce_sum | solution.py:82
  84.9 4.6 %convolution_convert_fusion.6 = bf16[256,1024]{1,0:T(8,128)(2,1)} fusion(bf16[256,2048]{1,0:T(8,128)(2,1)} %all-gather.2.cloned.1.call-done, bf16[1024,2048]{1,0:T(8,128)(2,1)} %param.11), kind=kOutput, calls=%fused_computation.35 | convolution fusion | flops 1074003968 | bytes 5767168 | tf_op jit(solution)/shard_map/dot_general | solution.py:40
  90.8 2.2 copy.155
  93.0 3.3 %fusion.9 = f32[256,8]{0,1:T(8,128)S(1)} fusion(f32[1,256,8,128]{1,3,2,0:T(8,128)} %bitcast.152, f32[8,256,128]{1,2,0:T(8,128)} %fusion.21, f32[8,256,128]{1,2,0:T(8,128)} %convolution_add_fusion.3, bf16[256,8,128]{0,2,1:T(8,128)(2,1)} %bitcast.155, f32[8,256,256]{1,2,0:T(8,128)} %get-tuple-element.22, f32[8,256]{1,0:T(8,128)S(1)} %log_add_fusion, ...), kind=kOutput, calls=%fused_computation.36 | convolution fusion | flops 136837120 | bytes 5783560 | tf_op jit(solution)/shard_map/bhij,bjhd->bihd/dot_general | solution.py:93
  110.4 2.2 fusion.8
  112.6 2.3 copy.128
  117.1 2.1 copy.112
  120.5 2.5 %copy.109 = f32[256,1024]{1,0:T(8,128)} copy(f32[256,1024]{0,1:T(8,128)} %bitcast.151) | data formatting | bytes 2097152 | tf_op jit(solution)/shard_map/reshape | solution.py:27
  123.1 2.1 copy.108
  128.7 2.1 convolution_convert_fusion.1
  133.2 2.1 convolution_convert_fusion.2
  141.6 11.0 %collective-permute-done.7 = bf16[256,1024]{1,0:T(8,128)(2,1)} collective-permute-done((bf16[256,1024]{1,0:T(8,128)(2,1)}, bf16[256,1024]{1,0:T(8,128)(2,1)}, u32[]{:S(2)}, u32[]{:S(2)}) %collective-permute-start.7) | collective-permute-done | bytes 524320 | tf_op jit(solution)/shard_map/ppermute | solution.py:17
  152.5 23.4 %collective-permute-done.6 = bf16[256,1024]{1,0:T(8,128)(2,1)} collective-permute-done((bf16[256,1024]{1,0:T(8,128)(2,1)}, bf16[256,1024]{1,0:T(8,128)(2,1)}, u32[]{:S(2)}, u32[]{:S(2)}) %collective-permute-start.6) | collective-permute-done | bytes 524320 | tf_op jit(solution)/shard_map/ppermute | solution.py:17
  176.0 2.5 %add_convert_fusion.1 = bf16[256,1024]{1,0:T(8,128)(2,1)} fusion(bf16[256,1024]{1,0:T(8,128)(2,1)} %collective-permute-done.8, bf16[256,1024]{1,0:T(8,128)(2,1)} %collective-permute-done.7, f32[256,1024]{1,0:T(8,128)S(1)} %copy-done.7, bf16[256,1024]{1,0:T(8,128)(2,1)} %collective-permute-done.6), kind=kLoop, calls=%fused_computation.38 | loop fusion | flops 1835008 | bytes 3145728 | tf_op jit(solution)/shard_map/convert_element_type | solution.py:139
  178.4 4.8 %collective-permute-done.10 = bf16[256,1024]{1,0:T(8,128)(2,1)} collective-permute-done((bf16[256,1024]{1,0:T(8,128)(2,1)}, bf16[256,1024]{1,0:T(8,128)(2,1)}, u32[]{:S(2)}, u32[]{:S(2)}) %collective-permute-start.10) | collective-permute-done | bytes 524320 | tf_op jit(solution)/shard_map/ppermute | solution.py:17
  183.2 35.6 %collective-permute-done.9 = bf16[256,1024]{1,0:T(8,128)(2,1)S(1)} collective-permute-done((bf16[256,1024]{1,0:T(8,128)(2,1)}, bf16[256,1024]{1,0:T(8,128)(2,1)S(1)}, u32[]{:S(2)}, u32[]{:S(2)}) %collective-permute-start.9) | collective-permute-done | bytes 524320 | tf_op jit(solution)/shard_map/ppermute | solution.py:17
  218.8 2.3 %add_convert_fusion = bf16[256,1024]{1,0:T(8,128)(2,1)} fusion(bf16[256,1024]{1,0:T(8,128)(2,1)} %collective-permute-done.11, bf16[256,1024]{1,0:T(8,128)(2,1)} %collective-permute-done.10, f32[256,1024]{1,0:T(8,128)S(1)} %copy.121, bf16[256,1024]{1,0:T(8,128)(2,1)S(1)} %collective-permute-done.9), kind=kLoop, calls=%fused_computation.37 | loop fusion | flops 1835008 | bytes 3145728 | tf_op jit(solution)/shard_map/convert_element_type | solution.py:140
  (89 shorter events, 44.9 us)
Async XLA Ops:
  7.2 12.6 %copy-start.19 = (bf16[256,1024]{1,0:T(8,128)(2,1)S(1)}, bf16[256,1024]{1,0:T(8,128)(2,1)}, u32[]{:S(2)}) copy-start(bf16[256,1024]{1,0:T(8,128)(2,1)} %param.7) | copy-start | bytes 1572868
  7.2 12.8 %copy-start.20 = (s32[1,3]{1,0:T(1,128)S(1)}, s32[1,3]{1,0:T(1,128)}, u32[]{:S(2)}) copy-start(s32[1,3]{1,0:T(1,128)} %param.13) | copy-start | bytes 40
  7.2 77.8 %all-gather.2.cloned.1.call-start = ((), (), s32[]{:S(2)}) async-start(), calls=%async_computation | async-start | bytes 1310720 | tf_op jit(solution)/shard_map/all_gather | solution.py:41
  8.5 23.0 %copy-start.5 = (bf16[256,1024]{0,1:T(8,128)(2,1)}, bf16[256,1024]{0,1:T(8,128)(2,1)S(1)}, u32[]{:S(2)}) copy-start(bf16[256,1024]{0,1:T(8,128)(2,1)S(1)} %copy.156) | copy-start | bytes 1572868
  8.5 17.2 %collective-permute-start = (bf16[256,1024]{0,1:T(8,128)(2,1)S(1)}, bf16[256,1024]{0,1:T(8,128)(2,1)}, u32[]{:S(2)}, u32[]{:S(2)}) collective-permute-start(bf16[256,1024]{0,1:T(8,128)(2,1)S(1)} %copy.156), channel_id=1, source_target_pairs={{0,4},{4,8},{8,12},{12,16},{16,20},{20,24},{24,28},{1,5},{5,9},{9,... | collective-permute-start | bytes 1572872 | tf_op jit(solution)/shard_map/ppermute | solution.py:17
  14.2 22.8 %collective-permute-start.3 = (bf16[256,1024]{1,0:T(8,128)(2,1)}, bf16[256,1024]{1,0:T(8,128)(2,1)}, u32[]{:S(2)}, u32[]{:S(2)}) collective-permute-start(bf16[256,1024]{1,0:T(8,128)(2,1)} %param.9), channel_id=1, source_target_pairs={{0,4},{4,8},{8,12},{12,16},{16,20},{20,24},{24,28},{1,5},{5,9},{9,... | collective-permute-start | bytes 1572872 | tf_op jit(solution)/shard_map/ppermute | solution.py:17
  19.8 22.4 %copy-start.21 = (s32[8,3]{0,1:T(4,128)S(1)}, s32[8,3]{0,1:T(4,128)}, u32[]{:S(2)}) copy-start(s32[8,3]{0,1:T(4,128)} %param.12) | copy-start | bytes 292
  25.7 22.6 %collective-permute-start.1 = (bf16[256,1024]{0,1:T(8,128)(2,1)}, bf16[256,1024]{0,1:T(8,128)(2,1)}, u32[]{:S(2)}, u32[]{:S(2)}) collective-permute-start(bf16[256,1024]{0,1:T(8,128)(2,1)} %collective-permute-done), channel_id=1, source_target_pairs={{0,4},{4,8},{8,12},{12,16},{16,20},{20,24},{24,28},{1,5},{5,9},{9,... | collective-permute-start | bytes 1572872 | tf_op jit(solution)/shard_map/ppermute | solution.py:17
  37.0 21.3 %collective-permute-start.4 = (bf16[256,1024]{1,0:T(8,128)(2,1)}, bf16[256,1024]{1,0:T(8,128)(2,1)}, u32[]{:S(2)}, u32[]{:S(2)}) collective-permute-start(bf16[256,1024]{1,0:T(8,128)(2,1)} %collective-permute-done.3), channel_id=1, source_target_pairs={{0,4},{4,8},{8,12},{12,16},{16,20},{20,24},{24,28},{1,5},{5,9},{9,... | collective-permute-start | bytes 1572872 | tf_op jit(solution)/shard_map/ppermute | solution.py:17
  48.3 22.4 %collective-permute-start.2 = (bf16[256,1024]{0,1:T(8,128)(2,1)}, bf16[256,1024]{0,1:T(8,128)(2,1)S(1)}, u32[]{:S(2)}, u32[]{:S(2)}) collective-permute-start(bf16[256,1024]{0,1:T(8,128)(2,1)} %collective-permute-done.1), channel_id=1, source_target_pairs={{0,8},{4,12},{8,16},{12,20},{16,24},{20,28},{1,9},{5,13},{9,17},{1... | collective-permute-start | bytes 1572872 | tf_op jit(solution)/shard_map/ppermute | solution.py:17
  58.4 16.0 %collective-permute-start.5 = (bf16[256,1024]{1,0:T(8,128)(2,1)}, bf16[256,1024]{1,0:T(8,128)(2,1)}, u32[]{:S(2)}, u32[]{:S(2)}) collective-permute-start(bf16[256,1024]{1,0:T(8,128)(2,1)} %collective-permute-done.4), channel_id=1, source_target_pairs={{0,8},{4,12},{8,16},{12,20},{16,24},{20,28},{1,9},{5,13},{9,17},{1... | collective-permute-start | bytes 1572872 | tf_op jit(solution)/shard_map/ppermute | solution.py:17
  70.7 1.9 copy-start.13
  75.6 6.7 %copy-start.11 = (bf16[256,1024]{0,1:T(8,128)(2,1)}, bf16[256,1024]{0,1:T(8,128)(2,1)S(1)}, u32[]{:S(2)}) copy-start(bf16[256,1024]{0,1:T(8,128)(2,1)S(1)} %copy.82) | copy-start | bytes 1572868
  75.6 4.6 %copy-start.3 = (f32[8,256,256]{1,2,0:T(8,128)S(1)}, f32[8,256,256]{1,2,0:T(8,128)}, u32[]{:S(2)}) copy-start(f32[8,256,256]{1,2,0:T(8,128)} %get-tuple-element.20) | copy-start | bytes 6291460
  75.6 4.6 %copy-start.15 = (bf16[256,1024]{0,1:T(8,128)(2,1)S(1)}, bf16[256,1024]{0,1:T(8,128)(2,1)}, u32[]{:S(2)}) copy-start(bf16[256,1024]{0,1:T(8,128)(2,1)} %copy.86) | copy-start | bytes 1572868
  80.2 1.6 copy-start.8
  81.8 1.6 copy-start
  93.0 3.3 %copy-start.4 = (f32[8,256,256]{1,2,0:T(8,128)S(1)}, f32[8,256,256]{1,2,0:T(8,128)}, u32[]{:S(2)}) copy-start(f32[8,256,256]{1,2,0:T(8,128)} %get-tuple-element.20) | copy-start | bytes 6291460
  93.0 3.4 %copy-start.16 = (bf16[256,1024]{0,1:T(8,128)(2,1)S(1)}, bf16[256,1024]{0,1:T(8,128)(2,1)}, u32[]{:S(2)}) copy-start(bf16[256,1024]{0,1:T(8,128)(2,1)} %copy.86) | copy-start | bytes 1572868
  97.5 1.7 copy-start.12
  99.1 1.7 copy-start.10
  101.6 2.7 %copy-start.6 = (bf16[256,1024]{0,1:T(8,128)(2,1)S(1)}, bf16[256,1024]{0,1:T(8,128)(2,1)}, u32[]{:S(2)}) copy-start(bf16[256,1024]{0,1:T(8,128)(2,1)} %copy-done.5) | copy-start | bytes 1572868
  106.1 2.7 %copy-start.14 = (bf16[256,1024]{0,1:T(8,128)(2,1)S(1)}, bf16[256,1024]{0,1:T(8,128)(2,1)}, u32[]{:S(2)}) copy-start(bf16[256,1024]{0,1:T(8,128)(2,1)} %copy-done.13) | copy-start | bytes 1572868
  110.4 4.5 %copy-start.18 = (bf16[8,256,128]{1,2,0:T(8,128)(2,1)S(1)}, bf16[8,256,128]{1,2,0:T(8,128)(2,1)}, u32[]{:S(2)}) copy-start(bf16[8,256,128]{1,2,0:T(8,128)(2,1)} %convolution_convert_fusion.3) | copy-start | bytes 1572868
  115.8 21.3 %collective-permute-start.8 = (bf16[256,1024]{1,0:T(8,128)(2,1)}, bf16[256,1024]{1,0:T(8,128)(2,1)}, u32[]{:S(2)}, u32[]{:S(2)}) collective-permute-start(bf16[256,1024]{1,0:T(8,128)(2,1)} %copy.115), channel_id=1, source_target_pairs={{4,0},{8,4},{12,8},{16,12},{20,16},{24,20},{28,24},{5,1},{9,5},{13... | collective-permute-start | bytes 1572872 | tf_op jit(solution)/shard_map/ppermute | solution.py:17
  117.1 9.3 %copy-start.17 = (bf16[8,128,256]{2,1,0:T(8,128)(2,1)S(1)}, bf16[8,128,256]{2,1,0:T(8,128)(2,1)}, u32[]{:S(2)}) copy-start(bf16[8,128,256]{2,1,0:T(8,128)(2,1)} %convolution_convert_fusion) | copy-start | bytes 1572868
  119.2 33.3 %collective-permute-start.7 = (bf16[256,1024]{1,0:T(8,128)(2,1)}, bf16[256,1024]{1,0:T(8,128)(2,1)}, u32[]{:S(2)}, u32[]{:S(2)}) collective-permute-start(bf16[256,1024]{1,0:T(8,128)(2,1)} %copy.112), channel_id=1, source_target_pairs={{8,0},{12,4},{16,8},{20,12},{24,16},{28,20},{9,1},{13,5},{17,9},{2... | collective-permute-start | bytes 1572872 | tf_op jit(solution)/shard_map/ppermute | solution.py:17
  125.2 50.8 %collective-permute-start.6 = (bf16[256,1024]{1,0:T(8,128)(2,1)}, bf16[256,1024]{1,0:T(8,128)(2,1)}, u32[]{:S(2)}, u32[]{:S(2)}) collective-permute-start(bf16[256,1024]{1,0:T(8,128)(2,1)} %copy.108), channel_id=1, source_target_pairs={{16,0},{20,4},{24,8},{28,12},{17,1},{21,5},{25,9},{29,13},{18,2},{... | collective-permute-start | bytes 1572872 | tf_op jit(solution)/shard_map/ppermute | solution.py:17
  127.5 51.0 %collective-permute-start.11 = (bf16[256,1024]{1,0:T(8,128)(2,1)}, bf16[256,1024]{1,0:T(8,128)(2,1)}, u32[]{:S(2)}, u32[]{:S(2)}) collective-permute-start(bf16[256,1024]{1,0:T(8,128)(2,1)} %copy.127), channel_id=1, source_target_pairs={{4,0},{8,4},{12,8},{16,12},{20,16},{24,20},{28,24},{5,1},{9,5},{13... | collective-permute-start | bytes 1572872 | tf_op jit(solution)/shard_map/ppermute | solution.py:17
  131.9 51.3 %collective-permute-start.10 = (bf16[256,1024]{1,0:T(8,128)(2,1)}, bf16[256,1024]{1,0:T(8,128)(2,1)}, u32[]{:S(2)}, u32[]{:S(2)}) collective-permute-start(bf16[256,1024]{1,0:T(8,128)(2,1)} %copy.124), channel_id=1, source_target_pairs={{8,0},{12,4},{16,8},{20,12},{24,16},{28,20},{9,1},{13,5},{17,9},{2... | collective-permute-start | bytes 1572872 | tf_op jit(solution)/shard_map/ppermute | solution.py:17
  137.1 81.7 %collective-permute-start.9 = (bf16[256,1024]{1,0:T(8,128)(2,1)}, bf16[256,1024]{1,0:T(8,128)(2,1)S(1)}, u32[]{:S(2)}, u32[]{:S(2)}) collective-permute-start(bf16[256,1024]{1,0:T(8,128)(2,1)} %copy.120), channel_id=1, source_target_pairs={{16,0},{20,4},{24,8},{28,12},{17,1},{21,5},{25,9},{29,13},{18,2},{... | collective-permute-start | bytes 1572872 | tf_op jit(solution)/shard_map/ppermute | solution.py:17
  139.9 36.0 %copy-start.7 = (f32[256,1024]{1,0:T(8,128)S(1)}, f32[256,1024]{1,0:T(8,128)}, u32[]{:S(2)}) copy-start(f32[256,1024]{1,0:T(8,128)} %copy.109) | copy-start | bytes 3145732
  (3 other events, 4.2 us)
Sparse Core Ops, SparseCore 0:
  14.4 16.2 all-gather.1
where the time goes:
time: 229 us; the launch traced here: 228 us
  waiting for transfers between devices  91.8 us (40%)
  starting transfers between devices  40.1 us (18%)
  matrix products  39.5 us (17%)
  local copies, waits for them, and re-layouts  30.9 us (13%)
  between operations  14.4 us (6%)
  other arithmetic  11.3 us (5%)
    ppermute x12, waiting for transfers between devices, shifted(): lax.ppermute(value, axis, [(source, source + steps) for source in range(i...  91.8 us
    ppermute x12, starting transfers between devices, shifted(): lax.ppermute(value, axis, [(source, source + steps) for source in range(i...  40.1 us
    dot_general x4, matrix products, body(): jnp.einsum('bihd,bjhd->bhij', query_blocks, key_entry[0], preferred_eleme...  8.23 us
    dot_general x4, matrix products, body(): jnp.einsum('bhij,bihd->bjhd', weight_list[set_index], grad_blocks, prefer...  7.14 us
    dot_general x4, matrix products, body(): jnp.einsum('bhij,bjhd->bihd', weight_set, key_entry[1], preferred_element...  6.93 us
    unnamed x45, local copies, waits for them, and re-layouts  5.54 us
    dot_general x4, matrix products, body(): jnp.einsum('bhij,bihd->bjhd', dlogit, query_blocks, preferred_element_typ...  5.36 us
    ppermute x3, local copies, waits for them, and re-layouts, shifted(): lax.ppermute(value, axis, [(source, source + steps) for source in range(i...  5.34 us
  transfers between devices with their start and end apart: 13, of which 10 were waited for; matrix products, arithmetic and copies ran while one was open for 20% of the time, Pallas kernels for 0%

commit v1 on v0

v1 whole, which is shorter than its diff:
```python
import functools
import math

import jax
import jax.numpy as jnp
from jax import lax
from jax.experimental import pallas as pl
from jax.experimental.pallas import tpu as pltpu
from jax.sharding import PartitionSpec as P

HDIM = 128
SECTIONS = 3
AHEAD = 2
MESH = pl.DeviceIdType.MESH
BF16 = jnp.bfloat16
F32 = jnp.float32


def dot(a, b, dims):
    return lax.dot_general(a, b, (dims, ((), ())), preferred_element_type=F32)


def kernel(
    count,
    lanes,
    q_ref,
    k_hbm,
    v_hbm,
    og_hbm,
    proj_hbm,
    table_ref,
    active_ref,
    dq_ref,
    dk_ref,
    dv_ref,
    kv,
    reach,
    term,
    back,
    own,
    og,
    proj,
    local_sem,
    load_sem,
    og_send,
    og_recv,
    fwd_send,
    fwd_recv,
    bwd_send,
    bwd_recv,
):
    heads, _, rows, _ = kv.shape
    width = og.shape[2]
    scale = 1.0 / math.sqrt(HDIM)
    quarter, eighth = count // 4, count // 8
    me = lax.axis_index("seq")
    lane = lax.axis_index("head")
    odd = (me // eighth) % 2 == 1
    even = jnp.logical_not(odd)
    up, down = me + quarter, me - quarter
    pair = jnp.where(odd, me - eighth, me + eighth)
    has_up, has_down = me < count - quarter, me >= quarter
    has_far = me >= 2 * quarter
    has_both = jnp.logical_and(has_up, has_down)
    odd_or_down = jnp.logical_or(odd, has_down)
    even_or_down = jnp.logical_or(even, has_down)
    twin = jnp.where(lane % 2 == 1, lane - 1, lane + 1)

    def cols(c):
        return pl.ds(pl.multiple_of(c * HDIM, HDIM), HDIM)

    def remote(src, dst, send, recv, axis, target):
        return pltpu.make_async_remote_copy(
            src_ref=src,
            dst_ref=dst,
            send_sem=send,
            recv_sem=recv,
            device_id={axis: target},
            device_id_type=MESH,
        )

    def fwd(kind, src, c, target):
        return remote(
            src.at[c], reach.at[kind, c], fwd_send.at[kind, c], fwd_recv.at[kind, c], "seq", target
        )

    def bwd(kind, c, target):
        return remote(
            term.at[kind, c],
            back.at[kind, c],
            bwd_send.at[kind, c],
            bwd_recv.at[kind, c],
            "seq",
            target,
        )

    def load_kv(c):
        return [
            pltpu.make_async_copy(src.at[:, cols(c)], kv.at[c, j], local_sem.at[j, c])
            for j, src in enumerate((k_hbm, v_hbm))
        ]

    load_og = pltpu.make_async_copy(og_hbm, og.at[lane], load_sem.at[0])
    load_proj = pltpu.make_async_copy(proj_hbm, proj, load_sem.at[1])
    load_og.start()

    @pl.loop(0, heads)
    def _(c):
        for copy in load_kv(c):
            copy.start()

    load_proj.start()

    barrier = pltpu.get_barrier_semaphore()
    peers = [lax.rem(lane + 2 * j, lanes) for j in range(1, lanes // 2)]
    for peer in [twin] + peers:
        pl.semaphore_signal(barrier, inc=1, device_id={"head": peer}, device_id_type=MESH)
    pl.semaphore_signal(barrier, inc=1, device_id={"seq": pair}, device_id_type=MESH)

    @pl.when(has_up)
    def _():
        pl.semaphore_signal(barrier, inc=1, device_id={"seq": up}, device_id_type=MESH)

    @pl.when(has_down)
    def _():
        pl.semaphore_signal(barrier, inc=1, device_id={"seq": down}, device_id_type=MESH)

    pl.semaphore_wait(
        barrier, 2 + len(peers) + has_up.astype(jnp.int32) + has_down.astype(jnp.int32)
    )

    def send_own(c):
        for copy in load_kv(c):
            copy.wait()

        @pl.when(has_up)
        def _():
            fwd(1, kv, c, up).start()

        @pl.when(even)
        def _():
            fwd(2, kv, c, pair).start()

    def forward(c):
        @pl.when(has_down)
        def _():
            fwd(1, kv, c, up).wait_recv()

        @pl.when(has_both)
        def _():
            fwd(0, reach.at[1], c, up).start()

        @pl.when(jnp.logical_and(odd, has_down))
        def _():
            fwd(2, reach.at[1], c, pair).start()

        @pl.when(c + AHEAD < heads)
        def _():
            send_own(c + AHEAD)

    def og_peer(index, slot, target):
        return remote(
            og.at[slot], og.at[slot], og_send.at[index], og_recv.at[slot], "head", target
        )

    load_og.wait()
    for j, peer in enumerate(peers):
        og_peer(1 + j, lane, peer).start()
    og_peer(0, lane, twin).start()
    for c in range(AHEAD):
        send_own(jnp.int32(c))

    for present, buffer in (
        (has_far, reach.at[0]),
        (has_down, reach.at[1]),
        (odd_or_down, reach.at[2]),
        (has_both, back.at[0]),
        (has_up, back.at[1]),
        (even_or_down, back.at[2]),
    ):

        @pl.when(jnp.logical_not(present))
        def _():
            @pl.loop(0, heads)
            def _(c):
                buffer[c] = jnp.zeros(buffer.shape[1:], BF16)

    forward(jnp.int32(0))
    for j, peer in enumerate(peers):
        og_peer(1 + j, peer, lane).wait_recv()
        og_peer(len(peers) + 1 + j, peer, twin).start()
    load_proj.wait()
    og_peer(0, twin, lane).wait_recv()
    for j in range(len(peers)):
        og_peer(len(peers) + 1 + j, lax.rem(twin + 2 * (j + 1), lanes), lane).wait_recv()

    key_index = lax.broadcasted_iota(jnp.int32, (rows, rows), 0)
    query_index = lax.broadcasted_iota(jnp.int32, (rows, rows), 1)

    def compute(c):
        grad = sum(
            dot(og[p], proj[cols(c), p * width : (p + 1) * width], ((1,), (1,)))
            for p in range(lanes)
        ).astype(BF16)
        query = q_ref[:, cols(c)]

        @pl.when(has_far)
        def _():
            fwd(0, kv, c, up).wait_recv()

        @pl.when(odd_or_down)
        def _():
            fwd(2, kv, c, pair).wait_recv()

        pieces = [(kv[c, 0], kv[c, 1])] + [
            (reach[k, c, 0], reach[k, c, 1]) for k in range(SECTIONS)
        ]
        logits = []
        for k, (key, _) in enumerate(pieces):
            raw = dot(key, query, ((1,), (1,))) * scale
            if k == 0:
                raw = jnp.where(key_index <= query_index, raw, -1e30)
            else:
                usable = jnp.logical_and(
                    table_ref[c, k - 1] * active_ref[0, k - 1] > 0, me >= count // 2**k
                )
                raw = raw + jnp.where(usable, 0.0, -1e30).astype(F32)
            logits.append(raw)
        top = functools.reduce(jnp.maximum, [jnp.max(x, axis=0, keepdims=True) for x in logits])
        exps = [jnp.exp(x - top) for x in logits]
        inverse = 1.0 / sum(jnp.sum(x, axis=0, keepdims=True) for x in exps)
        probs = [x * inverse for x in exps]
        weights = [x.astype(BF16) for x in probs]
        prob_grads = [dot(value, grad, ((1,), (1,))) for _, value in pieces]
        delta = sum(
            jnp.sum(w.astype(F32) * x, axis=0, keepdims=True) for w, x in zip(weights, prob_grads)
        )
        query_sum = None
        for k in (1, 3, 2, 0):
            dlogit = (probs[k] * (prob_grads[k] - delta) * scale).astype(BF16)
            key_term = dot(dlogit, query, ((1,), (0,)))
            value_term = dot(weights[k], grad, ((1,), (0,)))
            if k:
                term[k - 1, c, 0] = key_term.astype(BF16)
                term[k - 1, c, 1] = value_term.astype(BF16)
            else:
                own[c, 0] = key_term
                own[c, 1] = value_term
            part = dot(pieces[k][0], dlogit, ((0,), (0,)))
            query_sum = part if query_sum is None else query_sum + part

            if k == 1:

                @pl.when(has_far)
                def _():
                    bwd(0, c, down).start()

            if k == 3:

                @pl.when(odd_or_down)
                def _():
                    bwd(2, c, pair).start()

        dq_ref[:, cols(c)] = query_sum.T.astype(BF16)

    def merge(c):
        @pl.when(has_both)
        def _():
            bwd(0, c, down).wait_recv()

        @pl.when(even_or_down)
        def _():
            bwd(2, c, pair).wait_recv()

        @pl.when(has_down)
        def _():
            for j in range(2):
                side = jnp.where(odd, back[2, c, j].astype(F32), 0.0)
                total = term[1, c, j].astype(F32) + back[0, c, j].astype(F32) + side
                term[1, c, j] = total.astype(BF16)
            bwd(1, c, down).start()

    def finish(c):
        @pl.when(has_up)
        def _():
            bwd(1, c, down).wait_recv()

        for j, out in enumerate((dk_ref, dv_ref)):
            side = jnp.where(even, back[2, c, j].astype(F32), 0.0)
            out[:, cols(c)] = (own[c, j] + back[1, c, j].astype(F32) + side).astype(BF16)

    @pl.loop(0, heads + 2)
    def _(i):
        @pl.when(i + 1 < heads)
        def _():
            forward(i + 1)

        @pl.when(i < heads)
        def _():
            compute(i)

        @pl.when(jnp.logical_and(i >= 1, i <= heads))
        def _():
            merge(i - 1)

        @pl.when(i >= 2)
        def _():
            finish(i - 2)

    for index in range(lanes - 1):
        og_peer(index, lane, twin).wait_send()

    @pl.loop(0, heads)
    def _(c):
        for present, copy in (
            (has_both, fwd(0, kv, c, up)),
            (has_up, fwd(1, kv, c, up)),
            (even_or_down, fwd(2, kv, c, pair)),
            (has_far, bwd(0, c, down)),
            (has_down, bwd(1, c, down)),
            (odd_or_down, bwd(2, c, pair)),
        ):

            @pl.when(present)
            def _():
                copy.wait_send()


def body(count, lanes, queries, key_rows, value_rows, out_grad, out_proj, table, active):
    rows, columns = queries.shape
    heads = columns // HDIM
    block = (heads, 2, rows, HDIM)
    vmem = pl.BlockSpec(memory_space=pltpu.VMEM)
    smem = pl.BlockSpec(memory_space=pltpu.SMEM)
    hbm = pl.BlockSpec(memory_space=pl.ANY)
    dma = pltpu.SemaphoreType.DMA
    return pl.pallas_call(
        functools.partial(kernel, count, lanes),
        out_shape=[jax.ShapeDtypeStruct((rows, columns), BF16)] * 3,
        in_specs=[vmem, hbm, hbm, hbm, hbm, smem, smem],
        out_specs=[vmem] * 3,
        scratch_shapes=[
            pltpu.VMEM(block, BF16),
            pltpu.VMEM((SECTIONS,) + block, BF16),
            pltpu.VMEM((SECTIONS,) + block, BF16),
            pltpu.VMEM((SECTIONS,) + block, BF16),
            pltpu.VMEM(block, F32),
            pltpu.VMEM((lanes,) + out_grad.shape, BF16),
            pltpu.VMEM(out_proj.shape, BF16),
            dma((2, heads)),
            dma((2,)),
            dma((lanes,)),
            dma((lanes,)),
            dma((SECTIONS, heads)),
            dma((SECTIONS, heads)),
            dma((SECTIONS, heads)),
            dma((SECTIONS, heads)),
        ],
        compiler_params=pltpu.CompilerParams(
            collective_id=0, has_side_effects=True, vmem_limit_bytes=60 * 2**20
        ),
    )(queries, key_rows, value_rows, out_grad, out_proj, table, active)


def solution(mesh):
    return jax.shard_map(
        functools.partial(body, mesh.shape["seq"], mesh.shape["head"]),
        mesh=mesh,
        in_specs=(
            P("seq", "head"),
            P("seq", "head"),
            P("seq", "head"),
            P("seq", "head"),
            P("head", None),
            P("head", None),
            P("seq", None),
        ),
        out_specs=(P("seq", "head"), P("seq", "head"), P("seq", "head")),
        check_vma=False,
    )
```

time: 229 us -> 74.7 us (0.33)
  waiting for transfers between devices: 91.8 us -> 0 us
  Pallas kernels: 0 us -> 66.8 us
  starting transfers between devices: 40.1 us -> 0 us
  matrix products: 39.5 us -> 0 us
  local copies, waits for them, and re-layouts: 30.9 us -> 6.95 us
  between operations: 14.4 us -> 0.64 us
  other arithmetic: 11.3 us -> 0 us
    ppermute x12 -> x0, waiting for transfers between devices: 91.8 us -> none  [shifted(): lax.ppermute(value, axis, [(source, source + steps) for source in range(i...]
    pallas_call x0 -> x1, Pallas kernels: none -> 66.8 us  [body(): pl.pallas_call(functools.partial(kernel, count, lanes), out_shape=[jax.Sh...]
    ppermute x12 -> x0, starting transfers between devices: 40.1 us -> none  [shifted(): lax.ppermute(value, axis, [(source, source + steps) for source in range(i...]
    dot_general x25 -> x0, matrix products: 39.5 us -> none  [the longest x4 8.23 us: body(): jnp.einsum('bihd,bjhd->bhij', query_blocks, key_entry[0], preferred_eleme...]
    convert_element_type x7 -> x0, local copies, waits for them, and re-layouts: 10.5 us -> none  [the longest x3 5.2 us: body(): key_term = key_term.astype(jnp.bfloat16)]
    ppermute x3 -> x0, local copies, waits for them, and re-layouts: 5.34 us -> none  [shifted(): lax.ppermute(value, axis, [(source, source + steps) for source in range(i...]
    another operation x4 -> x0, local copies, waits for them, and re-layouts: 4.78 us -> none
    convert_element_type x2 -> x0, other arithmetic: 4.77 us -> none  [the longest x1 2.46 us: body(): key_sum.astype(jnp.bfloat16)]
  transfers between devices with their start and end apart: 13 -> 0, of which waited for: 10 -> 0; matrix products, arithmetic and copies ran while one was open for 20% -> 0% of each run, Pallas kernels for 0% -> 0%
where the time goes in v1:
time: 74.7 us; the launch traced here: 74.4 us
  Pallas kernels  66.8 us (89%)
  local copies, waits for them, and re-layouts  6.95 us (9%)
    pallas_call x1, Pallas kernels, body(): pl.pallas_call(functools.partial(kernel, count, lanes), out_shape=[jax.Sh...  66.8 us
    unnamed x4, local copies, waits for them, and re-layouts  6.95 us

profile of v1, /device:TPU:0, one launch (start us, length us, event | category | flops | bytes accessed | tf_op | source)
XLA Modules:
  0.0 74.4 jit_solution(9627561252484429193)
XLA Ops:
  0.6 1.3 %copy.10.table_ref = s32[8,3]{1,0:T(8,128)} copy(s32[8,3]{0,1:T(4,128)} %param.12) | data formatting | bytes 192 | tf_op args[5]
  2.0 66.8 %shard_map.94 = (bf16[256,1024]{1,0:T(8,128)(2,1)}, bf16[256,1024]{1,0:T(8,128)(2,1)}, bf16[256,1024]{1,0:T(8,128)(2,1)}) custom-call(bf16[256,1024]{1,0:T(8,128)(2,1)} %q_ref.1, bf16[256,1024]{1,0:T(8,128)(2,1)} %k_hbm.1, bf16[256,1024]{1,0:T(8,128)(2,1)} %v_hbm.1, bf16[256,512]{1,0:T(8,128)(2,1)} %og_hbm.1, bf16[1024,2048]{1,0:T(8,128)(2,1)} %proj_hbm.1, ...), custom_call_target="tpu_custom_call" | custom-call | tf_op jit(solution)/shard_map/pallas_call | solution.py:337
  68.7 1.9 %copy.14 = bf16[256,1024]{1,0:T(8,128)(2,1)} copy(bf16[256,1024]{1,0:T(8,128)(2,1)} %get-tuple-element.6) | data formatting | bytes 1048576
  70.6 1.9 %copy.15 = bf16[256,1024]{1,0:T(8,128)(2,1)} copy(bf16[256,1024]{1,0:T(8,128)(2,1)} %get-tuple-element.7) | data formatting | bytes 1048576
  72.5 1.9 %copy.16 = bf16[256,1024]{1,0:T(8,128)(2,1)} copy(bf16[256,1024]{1,0:T(8,128)(2,1)} %get-tuple-element.8) | data formatting | bytes 1048576

commit v2 on v1

--- a/solution.py
+++ b/solution.py
@@ -79,17 +79,22 @@
             device_id_type=MESH,
         )
 
-    def fwd(kind, src, c, target):
+    def fwd(kind, src, c, j, target):
         return remote(
-            src.at[c], reach.at[kind, c], fwd_send.at[kind, c], fwd_recv.at[kind, c], "seq", target
-        )
-
-    def bwd(kind, c, target):
+            src.at[c, j],
+            reach.at[kind, c, j],
+            fwd_send.at[kind, j, c],
+            fwd_recv.at[kind, j, c],
+            "seq",
+            target,
+        )
+
+    def bwd(kind, c, j, target):
         return remote(
-            term.at[kind, c],
-            back.at[kind, c],
-            bwd_send.at[kind, c],
-            bwd_recv.at[kind, c],
+            term.at[kind, c, j],
+            back.at[kind, c, j],
+            bwd_send.at[kind, j, c],
+            bwd_recv.at[kind, j, c],
             "seq",
             target,
         )
@@ -130,29 +135,31 @@
     )
 
     def send_own(c):
-        for copy in load_kv(c):
+        for j, copy in enumerate(load_kv(c)):
             copy.wait()
 
-        @pl.when(has_up)
-        def _():
-            fwd(1, kv, c, up).start()
-
-        @pl.when(even)
-        def _():
-            fwd(2, kv, c, pair).start()
+            @pl.when(has_up)
+            def _():
+                fwd(1, kv, c, j, up).start()
+
+            @pl.when(even)
+            def _():
+                fwd(2, kv, c, j, pair).start()
 
     def forward(c):
-        @pl.when(has_down)
-        def _():
-            fwd(1, kv, c, up).wait_recv()
-
-        @pl.when(has_both)
-        def _():
-            fwd(0, reach.at[1], c, up).start()
-
-        @pl.when(jnp.logical_and(odd, has_down))
-        def _():
-            fwd(2, reach.at[1], c, pair).start()
+        for j in range(2):
+
+            @pl.when(has_down)
+            def _():
+                fwd(1, kv, c, j, up).wait_recv()
+
+            @pl.when(has_both)
+            def _():
+                fwd(0, reach.at[1], c, j, up).start()
+
+            @pl.when(jnp.logical_and(odd, has_down))
+            def _():
+                fwd(2, reach.at[1], c, j, pair).start()
 
         @pl.when(c + AHEAD < heads)
         def _():
@@ -204,88 +211,102 @@
         ).astype(BF16)
         query = q_ref[:, cols(c)]
 
-        @pl.when(has_far)
-        def _():
-            fwd(0, kv, c, up).wait_recv()
-
-        @pl.when(odd_or_down)
-        def _():
-            fwd(2, kv, c, pair).wait_recv()
-
-        pieces = [(kv[c, 0], kv[c, 1])] + [
-            (reach[k, c, 0], reach[k, c, 1]) for k in range(SECTIONS)
-        ]
-        logits = []
-        for k, (key, _) in enumerate(pieces):
-            raw = dot(key, query, ((1,), (1,))) * scale
+        def key_of(k):
+            return reach[k - 1, c, 0] if k else kv[c, 0]
+
+        def logits_of(k):
+            raw = dot(key_of(k), query, ((1,), (1,))) * scale
             if k == 0:
-                raw = jnp.where(key_index <= query_index, raw, -1e30)
-            else:
-                usable = jnp.logical_and(
-                    table_ref[c, k - 1] * active_ref[0, k - 1] > 0, me >= count // 2**k
-                )
-                raw = raw + jnp.where(usable, 0.0, -1e30).astype(F32)
-            logits.append(raw)
-        top = functools.reduce(jnp.maximum, [jnp.max(x, axis=0, keepdims=True) for x in logits])
-        exps = [jnp.exp(x - top) for x in logits]
+                return jnp.where(key_index <= query_index, raw, -1e30)
+            usable = jnp.logical_and(
+                table_ref[k - 1, c] * active_ref[0, k - 1] > 0, me >= count // 2**k
+            )
+            return raw + jnp.where(usable, 0.0, -1e30).astype(F32)
+
+        def prob_grad_of(k):
+            value = reach[k - 1, c, 1] if k else kv[c, 1]
+            return dot(value, grad, ((1,), (1,)))
+
+        logits, prob_grads = {}, {}
+        for k in (0, 2):
+            logits[k], prob_grads[k] = logits_of(k), prob_grad_of(k)
+        for j in range(2):
+
+            @pl.when(odd_or_down)
+            def _():
+                fwd(2, kv, c, j, pair).wait_recv()
+
+        logits[3], prob_grads[3] = logits_of(3), prob_grad_of(3)
+        for j in range(2):
+
+            @pl.when(has_far)
+            def _():
+                fwd(0, kv, c, j, up).wait_recv()
+
+        logits[1], prob_grads[1] = logits_of(1), prob_grad_of(1)
+        sets = range(SECTIONS + 1)
+        top = functools.reduce(
+            jnp.maximum, [jnp.max(logits[k], axis=0, keepdims=True) for k in sets]
+        )
+        exps = [jnp.exp(logits[k] - top) for k in sets]
         inverse = 1.0 / sum(jnp.sum(x, axis=0, keepdims=True) for x in exps)
         probs = [x * inverse for x in exps]
         weights = [x.astype(BF16) for x in probs]
-        prob_grads = [dot(value, grad, ((1,), (1,))) for _, value in pieces]
+
+        def leave(k, j):
+            kind, go = {1: (0, has_far), 3: (2, odd_or_down)}.get(k, (None, None))
+            if kind is not None:
+
+                @pl.when(go)
+                def _():
+                    bwd(kind, c, j, pair if kind == 2 else down).start()
+
+        def keep(k, j, value):
+            if k:
+                term[k - 1, c, j] = value.astype(BF16)
+                leave(k, j)
+            else:
+                own[c, j] = value
+
+        order = (1, 3, 2, 0)
+        for k in order:
+            keep(k, 1, dot(weights[k], grad, ((1,), (0,))))
         delta = sum(
-            jnp.sum(w.astype(F32) * x, axis=0, keepdims=True) for w, x in zip(weights, prob_grads)
+            jnp.sum(weights[k].astype(F32) * prob_grads[k], axis=0, keepdims=True) for k in sets
         )
         query_sum = None
-        for k in (1, 3, 2, 0):
+        for k in order:
             dlogit = (probs[k] * (prob_grads[k] - delta) * scale).astype(BF16)
-            key_term = dot(dlogit, query, ((1,), (0,)))
-            value_term = dot(weights[k], grad, ((1,), (0,)))
-            if k:
-                term[k - 1, c, 0] = key_term.astype(BF16)
-                term[k - 1, c, 1] = value_term.astype(BF16)
-            else:
-                own[c, 0] = key_term
-                own[c, 1] = value_term
-            part = dot(pieces[k][0], dlogit, ((0,), (0,)))
+            keep(k, 0, dot(dlogit, query, ((1,), (0,))))
+            part = dot(key_of(k), dlogit, ((0,), (0,)))
             query_sum = part if query_sum is None else query_sum + part
-
-            if k == 1:
-
-                @pl.when(has_far)
-                def _():
-                    bwd(0, c, down).start()
-
-            if k == 3:
-
-                @pl.when(odd_or_down)
-                def _():
-                    bwd(2, c, pair).start()
-
         dq_ref[:, cols(c)] = query_sum.T.astype(BF16)
 
     def merge(c):
-        @pl.when(has_both)
-        def _():
-            bwd(0, c, down).wait_recv()
-
-        @pl.when(even_or_down)
-        def _():
-            bwd(2, c, pair).wait_recv()
-
-        @pl.when(has_down)
-        def _():
-            for j in range(2):
+        for j in (1, 0):
+
+            @pl.when(has_both)
+            def _():
+                bwd(0, c, j, down).wait_recv()
+
+            @pl.when(even_or_down)
+            def _():
+                bwd(2, c, j, pair).wait_recv()
+
+            @pl.when(has_down)
+            def _():
                 side = jnp.where(odd, back[2, c, j].astype(F32), 0.0)
                 total = term[1, c, j].astype(F32) + back[0, c, j].astype(F32) + side
                 term[1, c, j] = total.astype(BF16)
-            bwd(1, c, down).start()
+                bwd(1, c, j, down).start()
 
     def finish(c):
-        @pl.when(has_up)
-        def _():
-            bwd(1, c, down).wait_recv()
-
-        for j, out in enumerate((dk_ref, dv_ref)):
+        for j, out in ((1, dv_ref), (0, dk_ref)):
+
+            @pl.when(has_up)
+            def _():
+                bwd(1, c, j, down).wait_recv()
+
             side = jnp.where(even, back[2, c, j].astype(F32), 0.0)
             out[:, cols(c)] = (own[c, j] + back[1, c, j].astype(F32) + side).astype(BF16)
 
@@ -312,18 +333,62 @@
 
     @pl.loop(0, heads)
     def _(c):
-        for present, copy in (
-            (has_both, fwd(0, kv, c, up)),
-            (has_up, fwd(1, kv, c, up)),
-            (even_or_down, fwd(2, kv, c, pair)),
-            (has_far, bwd(0, c, down)),
-            (has_down, bwd(1, c, down)),
-            (odd_or_down, bwd(2, c, pair)),
-        ):
-
-            @pl.when(present)
-            def _():
-                copy.wait_send()
+        for j in range(2):
+            for present, copy in (
+                (has_both, fwd(0, kv, c, j, up)),
+                (has_up, fwd(1, kv, c, j, up)),
+                (even_or_down, fwd(2, kv, c, j, pair)),
+                (has_far, bwd(0, c, j, down)),
+                (has_down, bwd(1, c, j, down)),
+                (odd_or_down, bwd(2, c, j, pair)),
+            ):
+
+                @pl.when(present)
+                def _():
+                    copy.wait_send()
+
+
+def publish_kernel(parts, *refs):
+    number = (len(refs) - 2) // 2
+    sources, targets = refs[:number], refs[number : 2 * number]
+    held, sems = refs[2 * number :]
+    rows = sources[0].shape[0] // parts
+    pieces = [(a, p) for a in range(number) for p in range(parts)]
+
+    def fetch(a, p):
+        return pltpu.make_async_copy(
+            sources[a].at[pl.ds(p * rows, rows)], held.at[a, p], sems.at[0, a, p]
+        )
+
+    def store(a, p):
+        return pltpu.make_async_copy(
+            held.at[a, p], targets[a].at[pl.ds(p * rows, rows)], sems.at[1, a, p]
+        )
+
+    for piece in pieces:
+        fetch(*piece).start()
+    for piece in pieces:
+        fetch(*piece).wait()
+        store(*piece).start()
+    for piece in pieces:
+        store(*piece).wait()
+
+
+def publish(arrays, parts=2):
+    rows, columns = arrays[0].shape
+    hbm = pl.BlockSpec(memory_space=pl.ANY)
+    number = len(arrays)
+    return pl.pallas_call(
+        functools.partial(publish_kernel, parts),
+        out_shape=[jax.ShapeDtypeStruct(a.shape, a.dtype) for a in arrays],
+        in_specs=[hbm] * number,
+        out_specs=[hbm] * number,
+        scratch_shapes=[
+            pltpu.VMEM((number, parts, rows // parts, columns), arrays[0].dtype),
+            pltpu.SemaphoreType.DMA((2, number, parts)),
+        ],
+        compiler_params=pltpu.CompilerParams(vmem_limit_bytes=60 * 2**20),
+    )(*arrays)
 
 
 def body(count, lanes, queries, key_rows, value_rows, out_grad, out_proj, table, active):
@@ -334,7 +399,7 @@
     smem = pl.BlockSpec(memory_space=pltpu.SMEM)
     hbm = pl.BlockSpec(memory_space=pl.ANY)
     dma = pltpu.SemaphoreType.DMA
-    return pl.pallas_call(
+    grads = pl.pallas_call(
         functools.partial(kernel, count, lanes),
         out_shape=[jax.ShapeDtypeStruct((rows, columns), BF16)] * 3,
         in_specs=[vmem, hbm, hbm, hbm, hbm, smem, smem],
@@ -351,15 +416,16 @@
             dma((2,)),
             dma((lanes,)),
             dma((lanes,)),
-            dma((SECTIONS, heads)),
-            dma((SECTIONS, heads)),
-            dma((SECTIONS, heads)),
-            dma((SECTIONS, heads)),
+            dma((SECTIONS, 2, heads)),
+            dma((SECTIONS, 2, heads)),
+            dma((SECTIONS, 2, heads)),
+            dma((SECTIONS, 2, heads)),
         ],
         compiler_params=pltpu.CompilerParams(
             collective_id=0, has_side_effects=True, vmem_limit_bytes=60 * 2**20
         ),
-    )(queries, key_rows, value_rows, out_grad, out_proj, table, active)
+    )(queries, key_rows, value_rows, out_grad, out_proj, table.T, active)
+    return tuple(publish(grads))
 
 
 def solution(mesh):

time: 74.7 us -> 69.3 us (0.928)
  local copies, waits for them, and re-layouts: 6.95 us -> 0 us
  Pallas kernels: 66.8 us -> 68.4 us
    unnamed x4 -> x0, local copies, waits for them, and re-layouts: 6.95 us -> none
    pallas_call x0 -> x1, Pallas kernels: none -> 2.19 us  [publish(): pl.pallas_call(functools.partial(publish_kernel, parts), out_shape=[jax.S...]
where the time goes in v2:
time: 69.3 us; the launch traced here: 69 us
  Pallas kernels  68.4 us (99%)
    pallas_call x1, Pallas kernels, body(): pl.pallas_call(functools.partial(kernel, count, lanes), out_shape=[jax.Sh...  66.2 us
    pallas_call x1, Pallas kernels, publish(): pl.pallas_call(functools.partial(publish_kernel, parts), out_shape=[jax.S...  2.19 us

profile of v2, /device:TPU:0, one launch (start us, length us, event | category | flops | bytes accessed | tf_op | source)
XLA Modules:
  0.0 69.0 jit_solution(17819908481857308591)
XLA Ops:
  0.6 66.2 %shard_map.94 = (bf16[256,1024]{1,0:T(8,128)(2,1)}, bf16[256,1024]{1,0:T(8,128)(2,1)}, bf16[256,1024]{1,0:T(8,128)(2,1)}) custom-call(bf16[256,1024]{1,0:T(8,128)(2,1)} %q_ref.1, bf16[256,1024]{1,0:T(8,128)(2,1)} %k_hbm.1, bf16[256,1024]{1,0:T(8,128)(2,1)} %v_hbm.1, bf16[256,512]{1,0:T(8,128)(2,1)} %og_hbm.1, bf16[1024,2048]{1,0:T(8,128)(2,1)} %proj_hbm.1, ...), custom_call_target="tpu_custom_call" | custom-call | tf_op jit(solution)/shard_map/pallas_call | solution.py:402
  66.8 2.2 %shard_map.95 = (bf16[256,1024]{1,0:T(8,128)(2,1)}, bf16[256,1024]{1,0:T(8,128)(2,1)}, bf16[256,1024]{1,0:T(8,128)(2,1)}) custom-call(bf16[256,1024]{1,0:T(8,128)(2,1)} %get-tuple-element.6.refs_0_, bf16[256,1024]{1,0:T(8,128)(2,1)} %get-tuple-element.7.refs_1_, bf16[256,1024]{1,0:T(8,128)(2,1)} %get-tuple-element.8.refs_2_), custom_call_target="tpu_custom_call" | custom-call | tf_op jit(solution)/shard_map/pallas_call | solution.py:381

commit v3 on v2

--- a/solution.py
+++ b/solution.py
@@ -30,9 +30,9 @@
     proj_hbm,
     table_ref,
     active_ref,
-    dq_ref,
-    dk_ref,
-    dv_ref,
+    dq_hbm,
+    dk_hbm,
+    dv_hbm,
     kv,
     reach,
     term,
@@ -48,6 +48,8 @@
     fwd_recv,
     bwd_send,
     bwd_recv,
+    result,
+    out_sem,
 ):
     heads, _, rows, _ = kv.shape
     width = og.shape[2]
@@ -105,6 +107,12 @@
             for j, src in enumerate((k_hbm, v_hbm))
         ]
 
+    def write(index, c):
+        target = (dq_hbm, dk_hbm, dv_hbm)[index]
+        return pltpu.make_async_copy(
+            result.at[index, c], target.at[:, cols(c)], out_sem.at[index, c]
+        )
+
     load_og = pltpu.make_async_copy(og_hbm, og.at[lane], load_sem.at[0])
     load_proj = pltpu.make_async_copy(proj_hbm, proj, load_sem.at[1])
     load_og.start()
@@ -280,7 +288,8 @@
             keep(k, 0, dot(dlogit, query, ((1,), (0,))))
             part = dot(key_of(k), dlogit, ((0,), (0,)))
             query_sum = part if query_sum is None else query_sum + part
-        dq_ref[:, cols(c)] = query_sum.T.astype(BF16)
+        result[0, c] = query_sum.T.astype(BF16)
+        write(0, c).start()
 
     def merge(c):
         for j in (1, 0):
@@ -301,14 +310,15 @@
                 bwd(1, c, j, down).start()
 
     def finish(c):
-        for j, out in ((1, dv_ref), (0, dk_ref)):
+        for j in (1, 0):
 
             @pl.when(has_up)
             def _():
                 bwd(1, c, j, down).wait_recv()
 
             side = jnp.where(even, back[2, c, j].astype(F32), 0.0)
-            out[:, cols(c)] = (own[c, j] + back[1, c, j].astype(F32) + side).astype(BF16)
+            result[1 + j, c] = (own[c, j] + back[1, c, j].astype(F32) + side).astype(BF16)
+            write(1 + j, c).start()
 
     @pl.loop(0, heads + 2)
     def _(i):
@@ -333,6 +343,8 @@
 
     @pl.loop(0, heads)
     def _(c):
+        for index in range(3):
+            write(index, c).wait()
         for j in range(2):
             for present, copy in (
                 (has_both, fwd(0, kv, c, j, up)),
@@ -403,7 +415,7 @@
         functools.partial(kernel, count, lanes),
         out_shape=[jax.ShapeDtypeStruct((rows, columns), BF16)] * 3,
         in_specs=[vmem, hbm, hbm, hbm, hbm, smem, smem],
-        out_specs=[vmem] * 3,
+        out_specs=[hbm] * 3,
         scratch_shapes=[
             pltpu.VMEM(block, BF16),
             pltpu.VMEM((SECTIONS,) + block, BF16),
@@ -420,6 +432,8 @@
             dma((SECTIONS, 2, heads)),
             dma((SECTIONS, 2, heads)),
             dma((SECTIONS, 2, heads)),
+            pltpu.VMEM((3, heads, rows, HDIM), BF16),
+            dma((3, heads)),
         ],
         compiler_params=pltpu.CompilerParams(
             collective_id=0, has_side_effects=True, vmem_limit_bytes=60 * 2**20

time: 69.3 us -> 68.8 us (level)
  no operation moved by 1% of the time
where the time goes in v3:
time: 68.8 us; the launch traced here: 68.5 us
  Pallas kernels  67.9 us (99%)
    pallas_call x1, Pallas kernels, body(): pl.pallas_call(functools.partial(kernel, count, lanes), out_shape=[jax.Sh...  65.7 us
    pallas_call x1, Pallas kernels, publish(): pl.pallas_call(functools.partial(publish_kernel, parts), out_shape=[jax.S...  2.19 us

profile of v3, /device:TPU:0, one launch (start us, length us, event | category | flops | bytes accessed | tf_op | source)
XLA Modules:
  0.0 68.5 jit_solution(12203388231294157649)
XLA Ops:
  0.6 65.7 %shard_map.94 = (bf16[256,1024]{1,0:T(8,128)(2,1)}, bf16[256,1024]{1,0:T(8,128)(2,1)}, bf16[256,1024]{1,0:T(8,128)(2,1)}) custom-call(bf16[256,1024]{1,0:T(8,128)(2,1)} %q_ref.1, bf16[256,1024]{1,0:T(8,128)(2,1)} %k_hbm.1, bf16[256,1024]{1,0:T(8,128)(2,1)} %v_hbm.1, bf16[256,512]{1,0:T(8,128)(2,1)} %og_hbm.1, bf16[1024,2048]{1,0:T(8,128)(2,1)} %proj_hbm.1, ...), custom_call_target="tpu_custom_call" | custom-call | tf_op jit(solution)/shard_map/pallas_call | solution.py:414
  66.3 2.2 %shard_map.95 = (bf16[256,1024]{1,0:T(8,128)(2,1)}, bf16[256,1024]{1,0:T(8,128)(2,1)}, bf16[256,1024]{1,0:T(8,128)(2,1)}) custom-call(bf16[256,1024]{1,0:T(8,128)(2,1)} %get-tuple-element.6.refs_0_, bf16[256,1024]{1,0:T(8,128)(2,1)} %get-tuple-element.7.refs_1_, bf16[256,1024]{1,0:T(8,128)(2,1)} %get-tuple-element.8.refs_2_), custom_call_target="tpu_custom_call" | custom-call | tf_op jit(solution)/shard_map/pallas_call | solution.py:393
